TPU v7x, 128 devices: a whole 4x4x4 slice. The times are simulated.
128 devices in a mesh: gx: 16 (over z, y), gy: 8 (over x, core).
Axes of the slice: x: 4, y: 4, z: 4, core: 2. Of those that a mesh axis runs over, the one named last changes fastest.
Arguments:
- velocity_u: float32 [4, 2560, 2048], P(None, 'gy', 'gx'), may hold values from -6 to 6
- velocity_v: float32 [4, 2560, 2048], P(None, 'gy', 'gx'), may hold values from -6 to 6
- tracer: float32 [4, 2560, 2048], P(None, 'gy', 'gx'), may hold values from -6 to 6
- pressure_old: float32 [2560, 2048], P('gy', 'gx'), may hold values from -6 to 6
- depth: float32 [2560, 2048], P('gy', 'gx'), may hold values from 0.5 to 2
- helm: float32 [2560, 2048], P('gy', 'gx'), may hold values from 0.05 to 0.5
- land_mask: int32 [2560, 2048], P('gy', 'gx'), may hold values from 0 to 1, as said below
- clinic_map: int32 [64, 16], replicated, may hold values from 0 to 1, as said below
- tropic_map: int32 [64, 16], replicated, may hold values from -1 to 95, as said below
Outputs:
- velocity_u_new: float32 [4, 2560, 2048], P(None, 'gy', 'gx')
- velocity_v_new: float32 [4, 2560, 2048], P(None, 'gy', 'gx')
- tracer_new: float32 [4, 2560, 2048], P(None, 'gy', 'gx')
- pressure: float32 [2560, 2048], P('gy', 'gx')
Inputs may be any that keep to these rules, and one draw needn't show every extreme that they name: `land_mask`: rows 0 and 2559 are land; every column of a block whose tropic_map entry is -1 is land; every other block has an ocean column. `clinic_map`: 1 exactly on the blocks whose tropic_map entry is not -1. `tropic_map`: A quarter of the blocks of every device's clinic domain are -1. Another value t places the block in slot t % 6 of the device with gx index t // 6 and the gy index of the device that holds the block's rows; no slot is named twice. The blocks of one device's clinic domain place at most 1 block on any one device, and this bound is reached; every device receives at most 6 blocks, and this bound is reached.
All inputs are finite; a program needn't handle non-finite values.
Results may differ from a plain program's by a relative error of at most 0.00026.
Values sent between devices are 32-bit elements; how exact they have to be, the bound alone decides.
A program may use at most 64 MiB of HBM per device.

v0:
```python
import jax
import jax.numpy as jnp
from jax import lax
from jax.sharding import Mesh
from jax.sharding import PartitionSpec as P

BX = 128
BY = 40
ITERS = 4
GX_GY = ("gx_0", "gx_1", "gy_0", "gy_1")
GY = ("gy_0", "gy_1")
GX = ("gx_0", "gx_1")
step_time = 0.2
viscosity = 0.5
diffusivity = 0.5
vertical = 0.5
gravity = 1.0


def one_axis_at_a_time(x, axes):
    for axis in axes:
        x = lax.psum(x, axis)
    return x


def padded_2(cells, sides, width):
    for axis, dim in sides:
        count = lax.axis_size(axis)
        head = lax.slice_in_dim(cells, 0, width, axis=dim)
        tail = lax.slice_in_dim(cells, cells.shape[dim] - width, cells.shape[dim], axis=dim)
        cells = jnp.concatenate(
            [
                lax.ppermute(tail, axis, [(i, (i + 1) % count) for i in range(count)]),
                cells,
                lax.ppermute(head, axis, [((i + 1) % count, i) for i in range(count)]),
            ],
            axis=dim,
        )
    return cells


def padded_3(x, sides, width):
    edges = {}
    for axis, dim in sides:
        size, length = (lax.axis_size(axis), x.shape[dim])
        up = [(i, (i + 1) % size) for i in range(size)]
        last = lax.slice_in_dim(x, length - width, length, axis=dim)
        first = lax.slice_in_dim(x, 0, width, axis=dim)
        edges[dim] = (
            lax.ppermute(last, axis, up),
            lax.ppermute(first, axis, [(b, a) for a, b in up]),
        )
    done = []
    for _, dim in sides:
        low, high = edges[dim]
        around = [(width, width) if d in done else (0, 0) for d in range(x.ndim)]
        x = jnp.concatenate([jnp.pad(low, around), x, jnp.pad(high, around)], axis=dim)
        done.append(dim)
    return x


def beside_all(padded):
    centre = padded[..., 1:-1, 1:-1]
    return (
        centre,
        padded[..., 1:-1, 2:],
        padded[..., 1:-1, :-2],
        padded[..., 2:, 1:-1],
        padded[..., :-2, 1:-1],
    )


def faces(depths):
    centre, east_v, west_v, north_v, south_v = beside_all(depths)
    return (
        jnp.minimum(centre, east_v),
        jnp.minimum(centre, west_v),
        jnp.minimum(centre, north_v),
        jnp.minimum(centre, south_v),
    )


def diffuse(padded, coeffs):
    centre, east_v, west_v, north_v, south_v = beside_all(padded)
    face_e, face_w, face_n, face_s = coeffs
    return (
        face_e * (east_v - centre)
        + face_w * (west_v - centre)
        + face_n * (north_v - centre)
        + face_s * (south_v - centre)
    )


def mixing(field):
    diff = field[1:] - field[:-1]
    zero = jnp.zeros_like(field[:1])
    return jnp.concatenate([diff, zero], 0) - jnp.concatenate([zero, diff], 0)


def pair_totals(residual, precond, image):
    return (
        one_axis_at_a_time(jnp.sum(residual * precond), GX_GY),
        one_axis_at_a_time(jnp.sum(precond * image), GX_GY),
    )


def conjugate(apply, rhs, start, diagonal):
    solution = start
    residual = rhs - apply(start)
    precond = residual / diagonal
    image = apply(precond)
    rz_now, curve = pair_totals(residual, precond, image)
    alpha = rz_now / curve
    direction = precond
    along = image
    for step in range(ITERS):
        solution = solution + alpha * direction
        residual = residual - alpha * along
        if step + 1 < ITERS:
            precond = residual / diagonal
            image = apply(precond)
            rz_next, curve = pair_totals(residual, precond, image)
            ratio = rz_next / rz_now
            alpha = rz_next / (curve - ratio * rz_next / alpha)
            direction = precond + ratio * direction
            along = image + ratio * along
            rz_now = rz_next
    return solution


def on_device(
    velocity_u, velocity_v, tracer, pressure_old, depth, helm, land_mask, clinic_map, tropic_map
):
    f32 = jnp.float32
    levels, rows, cols = velocity_u.shape
    width_y = lax.axis_size(GY)
    col_dev = lax.axis_index(GX)
    row_dev = lax.axis_index(GY)
    per_y = rows // BY
    per_x = cols // BX
    total_rows = rows * width_y
    my_tropic = lax.dynamic_slice(tropic_map, (row_dev * per_y, col_dev * per_x), (per_y, per_x))
    my_clinic = lax.dynamic_slice(clinic_map, (row_dev * per_y, col_dev * per_x), (per_y, per_x))

    def spread(blockwise):
        return jnp.broadcast_to(blockwise[:, None, :, None], (per_y, BY, per_x, BX)).reshape(
            rows, cols
        )

    ocean = land_mask.astype(f32)
    domain = spread((my_tropic >= 0).astype(f32))
    active = spread(my_clinic.astype(f32))
    solve_mask = ocean * domain
    wet = depth * solve_mask
    stacked = jnp.concatenate([velocity_u, velocity_v, tracer, wet[None]], 0)
    padded = padded_2(stacked, ((GX, 2), (GY, 1)), 2)
    u_pad = padded[:levels]
    v_pad = padded[levels : 2 * levels]
    wet_pad = padded[3 * levels]
    cycle_faces = faces(wet_pad)
    inner_faces = tuple((face[1:-1, 1:-1] for face in cycle_faces))
    latitude = ((row_dev * rows - 1 + jnp.arange(rows + 2)) % total_rows).astype(f32)
    coriolis = (0.2 + 0.6 * ((latitude + 0.5) / total_rows)).reshape(rows + 2, 1)
    u_cycle = u_pad[:, 1:-1, 1:-1]
    v_cycle = v_pad[:, 1:-1, 1:-1]
    u_star = u_cycle + step_time * (
        vertical * mixing(u_cycle) + viscosity * diffuse(u_pad, cycle_faces) + coriolis * v_cycle
    )
    v_star = v_cycle + step_time * (
        vertical * mixing(v_cycle) + viscosity * diffuse(v_pad, cycle_faces) - coriolis * u_cycle
    )
    tracer_pad = padded[2 * levels : 3 * levels, 1:-1, 1:-1]
    _, tracer_e, tracer_w, tracer_n, tracer_s = beside_all(tracer_pad)
    tracer_raw = tracer + step_time * (
        vertical * mixing(tracer)
        + diffusivity * diffuse(tracer_pad, inner_faces)
        - 0.5 * (velocity_u * (tracer_e - tracer_w) + velocity_v * (tracer_n - tracer_s))
    )
    thick = ((2 * jnp.arange(levels) + 1).astype(f32) / (levels * levels)).reshape(levels, 1, 1)
    wet_cycle = wet_pad[1:-1, 1:-1]
    east_flow = wet_cycle * jnp.sum(thick * u_star, 0)
    north_flow = wet_cycle * jnp.sum(thick * v_star, 0)
    forcing = solve_mask * (
        -(east_flow[1:-1, 1:-1] - east_flow[1:-1, :-2])
        - (north_flow[1:-1, 1:-1] - north_flow[:-2, 1:-1])
    )
    face_e, face_w, face_n, face_s = inner_faces
    diagonal = helm + face_e + face_w + face_n + face_s
    start = solve_mask * pressure_old

    def plane_pad(field):
        return padded_3(field, ((GX, 1), (GY, 0)), 1)

    def apply_plane(field):
        _, east_v, west_v, north_v, south_v = beside_all(plane_pad(field))
        return (
            diagonal * field
            - face_e * east_v
            - face_w * west_v
            - face_n * north_v
            - face_s * south_v
        )

    pressure = conjugate(apply_plane, forcing, start, diagonal)
    _, east_p, _, north_p, _ = beside_all(plane_pad(pressure))
    grad_x = east_p - pressure
    grad_y = north_p - pressure
    keep_mask = active * ocean
    u_new = keep_mask * (u_star[:, 1:-1, 1:-1] - gravity * grad_x) + (1.0 - active) * velocity_u
    v_new = keep_mask * (v_star[:, 1:-1, 1:-1] - gravity * grad_y) + (1.0 - active) * velocity_v
    t_new = keep_mask * tracer_raw + (1.0 - active) * tracer
    return (u_new, v_new, t_new, pressure)


def solution(mesh):
    split = Mesh(mesh.devices.reshape(4, 4, 4, 2), ("gx_0", "gx_1", "gy_0", "gy_1"))
    in_specs = (
        P(None, GY, GX),
        P(None, GY, GX),
        P(None, GY, GX),
        P(GY, GX),
        P(GY, GX),
        P(GY, GX),
        P(GY, GX),
        P(),
        P(),
    )
    out_specs = (P(None, GY, GX), P(None, GY, GX), P(None, GY, GX), P(GY, GX))
    return jax.shard_map(
        on_device, mesh=split, in_specs=in_specs, out_specs=out_specs, check_vma=False
    )
```

profile of v0, /device:TPU:0, one launch (start us, length us, event | category | flops | bytes accessed | tf_op | source)
XLA Modules:
  0.0 265.8 jit_solution(10132375841164672830)
XLA Ops:
  9.5 6.7 %collective-permute-start.1 = (f32[13,320,2]{1,2,0:T(2,128)S(1)}, f32[13,320,2]{1,2,0:T(2,128)S(1)}, u32[]{:S(2)}, u32[]{:S(2)}) collective-permute-start(f32[13,320,2]{1,2,0:T(2,128)S(1)} %get-tuple-element.73), channel_id=1, source_target_pairs={{8,0},{16,8},{24,16},{32,24},{40,32},{48,40},{56,48},{64,56},{72,6... | collective-permute-start | bytes 99848 | tf_op jit(solution)/shard_map/ppermute | solution.py:35
  16.8 5.3 %collective-permute-start.4 = (f32[320,1]{0,1:T(1,128)}, f32[320,1]{0,1:T(1,128)}, u32[]{:S(2)}, u32[]{:S(2)}) collective-permute-start(f32[320,1]{0,1:T(1,128)} %get-tuple-element.108), channel_id=1, source_target_pairs={{8,0},{16,8},{24,16},{32,24},{40,32},{48,40},{56,48},{64,56},{72,6... | collective-permute-start | bytes 3848 | tf_op jit(solution)/shard_map/ppermute | solution.py:51
  24.8 2.3 copy.42
  27.1 2.3 collective-permute-start.3
  32.8 3.0 %collective-permute-start.6 = (f32[1,128]{0,1:T(8,128)}, f32[1,128]{0,1:T(8,128)}, u32[]{:S(2)}, u32[]{:S(2)}) collective-permute-start(f32[1,128]{0,1:T(8,128)} %get-tuple-element.105), channel_id=1, source_target_pairs={{1,0},{2,1},{3,2},{4,3},{5,4},{6,5},{7,6},{0,7},{9,8},{10,9},{11,1... | collective-permute-start | bytes 1544 | tf_op jit(solution)/shard_map/ppermute | solution.py:51
  38.9 2.3 pad_maximum_fusion
  42.5 8.3 %multiply_reduce_fusion.1 = (f32[322,130]{0,1:T(8,128)S(1)}, f32[322,130]{0,1:T(8,128)S(1)}, f32[4,322,130]{1,2,0:T(8,128)}, f32[4,322,130]{1,2,0:T(8,128)}) fusion(f32[4]{0:T(128)S(1)} %copy-done.28, f32[13,324,132]{1,2,0:T(8,128)S(1)} %pad_maximum_fusion, f32[322]{0:T(512)S(1)} %fusion.91, f32[13,320,2]{1,2,0:T(2,128)S(1)} %collective-permute-done.1, ...), kind=kLoop, calls=%fused_computation.40 | loop fusion | flops 10632440 | bytes 9592600 | tf_op jit(solution)/shard_map/reduce_sum | solution.py:181
  52.5 5.4 %collective-permute-start.8 = (f32[320,1]{0,1:T(1,128)S(1)}, f32[320,1]{0,1:T(1,128)S(1)}, u32[]{:S(2)}, u32[]{:S(2)}) collective-permute-start(f32[320,1]{0,1:T(1,128)S(1)} %get-tuple-element.104), channel_id=1, source_target_pairs={{8,0},{16,8},{24,16},{32,24},{40,32},{48,40},{56,48},{64,56},{72,6... | collective-permute-start | bytes 3848 | tf_op jit(solution)/shard_map/ppermute | solution.py:51
  58.0 3.0 %collective-permute-start.10 = (f32[1,128]{0,1:T(8,128)S(1)}, f32[1,128]{0,1:T(8,128)S(1)}, u32[]{:S(2)}, u32[]{:S(2)}) collective-permute-start(f32[1,128]{0,1:T(8,128)S(1)} %get-tuple-element.101), channel_id=1, source_target_pairs={{1,0},{2,1},{3,2},{4,3},{5,4},{6,5},{7,6},{0,7},{9,8},{10,9},{11,1... | collective-permute-start | bytes 1544 | tf_op jit(solution)/shard_map/ppermute | solution.py:51
  66.6 8.4 %all-reduce.28 = (f32[]{:T(128)}, f32[]{:T(128)}) all-reduce(f32[]{:T(128)} %get-tuple-element.19, f32[]{:T(128)} %get-tuple-element.18), channel_id=1, replica_groups=mesh['gx_0'=4,'gx_1'=4,'gy_0'=4,'gy_1'=2] {'gx_0'}, use_global_device_ids=true, to_apply=%region_3.4 | all-reduce | flops 2 | bytes 16 | tf_op jit(solution)/shard_map/psum | solution.py:22
  75.0 12.4 %all-reduce.24 = (f32[]{:T(128)}, f32[]{:T(128)}) all-reduce(f32[]{:T(128)} %get-tuple-element.44, f32[]{:T(128)} %get-tuple-element.45), channel_id=1, replica_groups=mesh['gx_0'=4,'gx_1'=4,'gy_0'=4,'gy_1'=2] {'gx_1'}, use_global_device_ids=true, to_apply=%region_4.5 | all-reduce | flops 2 | bytes 16 | tf_op jit(solution)/shard_map/psum | solution.py:22
  87.3 8.4 %all-reduce.20 = (f32[]{:T(128)}, f32[]{:T(128)}) all-reduce(f32[]{:T(128)} %get-tuple-element.36, f32[]{:T(128)} %get-tuple-element.37), channel_id=1, replica_groups=mesh['gx_0'=4,'gx_1'=4,'gy_0'=4,'gy_1'=2] {'gy_0'}, use_global_device_ids=true, to_apply=%region_5.6 | all-reduce | flops 2 | bytes 16 | tf_op jit(solution)/shard_map/psum | solution.py:22
  95.7 3.1 %all-reduce.32 = (f32[]{:T(128)}, f32[]{:T(128)}) all-reduce(f32[]{:T(128)} %get-tuple-element.28, f32[]{:T(128)} %get-tuple-element.29), channel_id=1, replica_groups=mesh['gx_0'=4,'gx_1'=4,'gy_0'=4,'gy_1'=2] {'gy_1'}, use_global_device_ids=true, to_apply=%region_6.7 | all-reduce | flops 2 | bytes 16 | tf_op jit(solution)/shard_map/psum | solution.py:22
  103.4 3.0 %collective-permute-start.14 = (f32[1,128]{0,1:T(8,128)S(1)}, f32[1,128]{0,1:T(8,128)S(1)}, u32[]{:S(2)}, u32[]{:S(2)}) collective-permute-start(f32[1,128]{0,1:T(8,128)S(1)} %get-tuple-element.97), channel_id=1, source_target_pairs={{1,0},{2,1},{3,2},{4,3},{5,4},{6,5},{7,6},{0,7},{9,8},{10,9},{11,1... | collective-permute-start | bytes 1544 | tf_op jit(solution)/shard_map/ppermute | solution.py:51
  108.3 3.0 %multiply_reduce_fusion.5 = (f32[]{:T(128)}, f32[]{:T(128)}, f32[320,128]{0,1:T(8,128)}) fusion(f32[320,128]{0,1:T(8,128)S(1)} %get-tuple-element.60, f32[320,128]{0,1:T(8,128)S(1)} %get-tuple-element.61, f32[320,1]{0,1:T(1,128)S(1)} %collective-permute-done.12, f32[320,1]{0,1:T(1,128)S(1)} %collective-permute-done.13, ...), kind=kLoop, calls=%fused_computation.190 | loop fusion | flops 1105918 | bytes 1314312 | tf_op jit(solution)/shard_map/reduce_sum | solution.py:103
  111.3 8.4 %all-reduce.27 = (f32[]{:T(128)}, f32[]{:T(128)}) all-reduce(f32[]{:T(128)} %get-tuple-element.17, f32[]{:T(128)} %get-tuple-element.16), channel_id=1, replica_groups=mesh['gx_0'=4,'gx_1'=4,'gy_0'=4,'gy_1'=2] {'gx_0'}, use_global_device_ids=true, to_apply=%region_13.14 | all-reduce | flops 2 | bytes 16 | tf_op jit(solution)/shard_map/psum | solution.py:22
  119.7 12.4 %all-reduce.23 = (f32[]{:T(128)}, f32[]{:T(128)}) all-reduce(f32[]{:T(128)} %get-tuple-element.42, f32[]{:T(128)} %get-tuple-element.43), channel_id=1, replica_groups=mesh['gx_0'=4,'gx_1'=4,'gy_0'=4,'gy_1'=2] {'gx_1'}, use_global_device_ids=true, to_apply=%region_14.15 | all-reduce | flops 2 | bytes 16 | tf_op jit(solution)/shard_map/psum | solution.py:22
  132.1 9.2 %all-reduce.19 = (f32[]{:T(128)}, f32[]{:T(128)}) all-reduce(f32[]{:T(128)} %get-tuple-element.34, f32[]{:T(128)} %get-tuple-element.35), channel_id=1, replica_groups=mesh['gx_0'=4,'gx_1'=4,'gy_0'=4,'gy_1'=2] {'gy_0'}, use_global_device_ids=true, to_apply=%region_15.16 | all-reduce | flops 2 | bytes 16 | tf_op jit(solution)/shard_map/psum | solution.py:22
  141.3 3.1 %all-reduce.31 = (f32[]{:T(128)}, f32[]{:T(128)}) all-reduce(f32[]{:T(128)} %get-tuple-element.26, f32[]{:T(128)} %get-tuple-element.27), channel_id=1, replica_groups=mesh['gx_0'=4,'gx_1'=4,'gy_0'=4,'gy_1'=2] {'gy_1'}, use_global_device_ids=true, to_apply=%region_16.17 | all-reduce | flops 2 | bytes 16 | tf_op jit(solution)/shard_map/psum | solution.py:22
  152.3 3.0 %collective-permute-start.18 = (f32[1,128]{0,1:T(8,128)S(1)}, f32[1,128]{0,1:T(8,128)S(1)}, u32[]{:S(2)}, u32[]{:S(2)}) collective-permute-start(f32[1,128]{0,1:T(8,128)S(1)} %get-tuple-element.93), channel_id=1, source_target_pairs={{1,0},{2,1},{3,2},{4,3},{5,4},{6,5},{7,6},{0,7},{9,8},{10,9},{11,1... | collective-permute-start | bytes 1544 | tf_op jit(solution)/shard_map/ppermute | solution.py:51
  159.6 8.4 %all-reduce.26 = (f32[]{:T(128)}, f32[]{:T(128)}) all-reduce(f32[]{:T(128)} %get-tuple-element.15, f32[]{:T(128)} %get-tuple-element.14), channel_id=1, replica_groups=mesh['gx_0'=4,'gx_1'=4,'gy_0'=4,'gy_1'=2] {'gx_0'}, use_global_device_ids=true, to_apply=%region_23.24 | all-reduce | flops 2 | bytes 16 | tf_op jit(solution)/shard_map/psum | solution.py:22
  168.0 12.3 %all-reduce.22 = (f32[]{:T(128)}, f32[]{:T(128)}) all-reduce(f32[]{:T(128)} %get-tuple-element.40, f32[]{:T(128)} %get-tuple-element.41), channel_id=1, replica_groups=mesh['gx_0'=4,'gx_1'=4,'gy_0'=4,'gy_1'=2] {'gx_1'}, use_global_device_ids=true, to_apply=%region_24.25 | all-reduce | flops 2 | bytes 16 | tf_op jit(solution)/shard_map/psum | solution.py:22
  180.3 8.4 %all-reduce.18 = (f32[]{:T(128)}, f32[]{:T(128)}) all-reduce(f32[]{:T(128)} %get-tuple-element.32, f32[]{:T(128)} %get-tuple-element.33), channel_id=1, replica_groups=mesh['gx_0'=4,'gx_1'=4,'gy_0'=4,'gy_1'=2] {'gy_0'}, use_global_device_ids=true, to_apply=%region_25.26 | all-reduce | flops 2 | bytes 16 | tf_op jit(solution)/shard_map/psum | solution.py:22
  188.7 3.1 %all-reduce.30 = (f32[]{:T(128)}, f32[]{:T(128)}) all-reduce(f32[]{:T(128)} %get-tuple-element.24, f32[]{:T(128)} %get-tuple-element.25), channel_id=1, replica_groups=mesh['gx_0'=4,'gx_1'=4,'gy_0'=4,'gy_1'=2] {'gy_1'}, use_global_device_ids=true, to_apply=%region_26.27 | all-reduce | flops 2 | bytes 16 | tf_op jit(solution)/shard_map/psum | solution.py:22
  208.7 8.3 %all-reduce.25 = (f32[]{:T(128)}, f32[]{:T(128)}) all-reduce(f32[]{:T(128)} %get-tuple-element.13, f32[]{:T(128)} %get-tuple-element.12), channel_id=1, replica_groups=mesh['gx_0'=4,'gx_1'=4,'gy_0'=4,'gy_1'=2] {'gx_0'}, use_global_device_ids=true, to_apply=%region_33.34 | all-reduce | flops 2 | bytes 16 | tf_op jit(solution)/shard_map/psum | solution.py:22
  217.1 12.5 %all-reduce.21 = (f32[]{:T(128)}, f32[]{:T(128)}) all-reduce(f32[]{:T(128)} %get-tuple-element.38, f32[]{:T(128)} %get-tuple-element.39), channel_id=1, replica_groups=mesh['gx_0'=4,'gx_1'=4,'gy_0'=4,'gy_1'=2] {'gx_1'}, use_global_device_ids=true, to_apply=%region_34.35 | all-reduce | flops 2 | bytes 16 | tf_op jit(solution)/shard_map/psum | solution.py:22
  229.6 9.1 %all-reduce.17 = (f32[]{:T(128)}, f32[]{:T(128)}) all-reduce(f32[]{:T(128)} %get-tuple-element.30, f32[]{:T(128)} %get-tuple-element.31), channel_id=1, replica_groups=mesh['gx_0'=4,'gx_1'=4,'gy_0'=4,'gy_1'=2] {'gy_0'}, use_global_device_ids=true, to_apply=%region_35.36 | all-reduce | flops 2 | bytes 16 | tf_op jit(solution)/shard_map/psum | solution.py:22
  238.7 3.1 %all-reduce.29 = (f32[]{:T(128)}, f32[]{:T(128)}) all-reduce(f32[]{:T(128)} %get-tuple-element.22, f32[]{:T(128)} %get-tuple-element.23), channel_id=1, replica_groups=mesh['gx_0'=4,'gx_1'=4,'gy_0'=4,'gy_1'=2] {'gy_1'}, use_global_device_ids=true, to_apply=%region_36.37 | all-reduce | flops 2 | bytes 16 | tf_op jit(solution)/shard_map/psum | solution.py:22
  251.3 4.4 %multiply_add_fusion = f32[4,320,128]{1,2,0:T(8,128)} fusion(f32[4,320,128]{1,2,0:T(8,128)S(1)} %copy.40, f32[4,320,128]{1,2,0:T(8,128)S(1)} %copy.39, f32[4,320,128]{1,2,0:T(8,128)S(1)} %copy.38, f32[13,320,2]{1,2,0:T(2,128)S(1)} %collective-permute-done.1, f32[1,320,128]{1,2,0:T(8,128)} %copy-done.13, f32[13,320,2]{1,2,0:T(2,128)S(1)} %collective-permute-done, ...), kind=kLoop, calls=%fused_computation.67 | loop fusion | flops 7536640 | bytes 4191296 | tf_op jit(solution)/shard_map/add | solution.py:211
  255.7 2.3 copy.63
  259.8 2.6 fusion.25
  262.5 2.2 copy.61
  (158 shorter events, 61.4 us)
Async XLA Ops:
  9.5 32.9 %copy-start.13 = (f32[1,320,128]{1,2,0:T(8,128)}, f32[1,320,128]{1,2,0:T(8,128)S(1)}, u32[]{:S(2)}) copy-start(f32[1,320,128]{1,2,0:T(8,128)S(1)} %get-tuple-element.83) | copy-start | bytes 491524
  9.5 13.3 %collective-permute-start.1 = (f32[13,320,2]{1,2,0:T(2,128)S(1)}, f32[13,320,2]{1,2,0:T(2,128)S(1)}, u32[]{:S(2)}, u32[]{:S(2)}) collective-permute-start(f32[13,320,2]{1,2,0:T(2,128)S(1)} %get-tuple-element.73), channel_id=1, source_target_pairs={{8,0},{16,8},{24,16},{32,24},{40,32},{48,40},{56,48},{64,56},{72,6... | collective-permute-start | bytes 99848 | tf_op jit(solution)/shard_map/ppermute | solution.py:35
  16.2 7.3 %collective-permute-start = (f32[13,320,2]{1,2,0:T(2,128)S(1)}, f32[13,320,2]{1,2,0:T(2,128)S(1)}, u32[]{:S(2)}, u32[]{:S(2)}) collective-permute-start(f32[13,320,2]{1,2,0:T(2,128)S(1)} %get-tuple-element.72), channel_id=1, source_target_pairs={{0,8},{8,16},{16,24},{24,32},{32,40},{40,48},{48,56},{56,64},{64,7... | collective-permute-start | bytes 99848 | tf_op jit(solution)/shard_map/ppermute | solution.py:33
  16.8 34.2 %collective-permute-start.4 = (f32[320,1]{0,1:T(1,128)}, f32[320,1]{0,1:T(1,128)}, u32[]{:S(2)}, u32[]{:S(2)}) collective-permute-start(f32[320,1]{0,1:T(1,128)} %get-tuple-element.108), channel_id=1, source_target_pairs={{8,0},{16,8},{24,16},{32,24},{40,32},{48,40},{56,48},{64,56},{72,6... | collective-permute-start | bytes 3848 | tf_op jit(solution)/shard_map/ppermute | solution.py:51
  22.1 28.8 %collective-permute-start.5 = (f32[320,1]{0,1:T(1,128)}, f32[320,1]{0,1:T(1,128)}, u32[]{:S(2)}, u32[]{:S(2)}) collective-permute-start(f32[320,1]{0,1:T(1,128)} %get-tuple-element.107), channel_id=1, source_target_pairs={{0,8},{8,16},{16,24},{24,32},{32,40},{40,48},{48,56},{56,64},{64,7... | collective-permute-start | bytes 3848 | tf_op jit(solution)/shard_map/ppermute | solution.py:50
  22.9 28.1 %collective-permute-start.7 = (f32[1,128]{0,1:T(8,128)}, f32[1,128]{0,1:T(8,128)}, u32[]{:S(2)}, u32[]{:S(2)}) collective-permute-start(f32[1,128]{0,1:T(8,128)} %get-tuple-element.106), channel_id=1, source_target_pairs={{0,1},{1,2},{2,3},{3,4},{4,5},{5,6},{6,7},{7,0},{8,9},{9,10},{10,1... | collective-permute-start | bytes 1544 | tf_op jit(solution)/shard_map/ppermute | solution.py:50
  27.1 5.8 %collective-permute-start.3 = (f32[13,2,132]{2,1,0:T(2,128)}, f32[13,2,132]{2,1,0:T(2,128)}, u32[]{:S(2)}, u32[]{:S(2)}) collective-permute-start(f32[13,2,132]{2,1,0:T(2,128)} %copy.42), channel_id=1, source_target_pairs={{1,0},{2,1},{3,2},{4,3},{5,4},{6,5},{7,6},{0,7},{9,8},{10,9},{11,1... | collective-permute-start | bytes 41192 | tf_op jit(solution)/shard_map/ppermute | solution.py:35
  30.5 6.4 %collective-permute-start.2 = (f32[13,2,132]{2,1,0:T(2,128)}, f32[13,2,132]{2,1,0:T(2,128)}, u32[]{:S(2)}, u32[]{:S(2)}) collective-permute-start(f32[13,2,132]{2,1,0:T(2,128)} %copy.41), channel_id=1, source_target_pairs={{0,1},{1,2},{2,3},{3,4},{4,5},{5,6},{6,7},{7,0},{8,9},{9,10},{10,1... | collective-permute-start | bytes 41192 | tf_op jit(solution)/shard_map/ppermute | solution.py:33
  32.8 18.1 %collective-permute-start.6 = (f32[1,128]{0,1:T(8,128)}, f32[1,128]{0,1:T(8,128)}, u32[]{:S(2)}, u32[]{:S(2)}) collective-permute-start(f32[1,128]{0,1:T(8,128)} %get-tuple-element.105), channel_id=1, source_target_pairs={{1,0},{2,1},{3,2},{4,3},{5,4},{6,5},{7,6},{0,7},{9,8},{10,9},{11,1... | collective-permute-start | bytes 1544 | tf_op jit(solution)/shard_map/ppermute | solution.py:51
  42.4 22.5 %copy-start.1 = (f32[322,130]{0,1:T(8,128)}, f32[322,130]{0,1:T(8,128)S(1)}, u32[]{:S(2)}) copy-start(f32[322,130]{0,1:T(8,128)S(1)} %get-tuple-element.76) | copy-start | bytes 502324
  42.4 22.5 %copy-start.4 = (f32[322,130]{0,1:T(8,128)}, f32[322,130]{0,1:T(8,128)S(1)}, u32[]{:S(2)}) copy-start(f32[322,130]{0,1:T(8,128)S(1)} %get-tuple-element.77) | copy-start | bytes 502324
  42.4 22.5 %copy-start.7 = (f32[322,130]{0,1:T(8,128)}, f32[322,130]{0,1:T(8,128)S(1)}, u32[]{:S(2)}) copy-start(f32[322,130]{0,1:T(8,128)S(1)} %get-tuple-element.78) | copy-start | bytes 502324
  42.4 22.5 %copy-start.10 = (f32[322,130]{0,1:T(8,128)}, f32[322,130]{0,1:T(8,128)S(1)}, u32[]{:S(2)}) copy-start(f32[322,130]{0,1:T(8,128)S(1)} %get-tuple-element.79) | copy-start | bytes 502324
  52.5 10.4 %collective-permute-start.8 = (f32[320,1]{0,1:T(1,128)S(1)}, f32[320,1]{0,1:T(1,128)S(1)}, u32[]{:S(2)}, u32[]{:S(2)}) collective-permute-start(f32[320,1]{0,1:T(1,128)S(1)} %get-tuple-element.104), channel_id=1, source_target_pairs={{8,0},{16,8},{24,16},{32,24},{40,32},{48,40},{56,48},{64,56},{72,6... | collective-permute-start | bytes 3848 | tf_op jit(solution)/shard_map/ppermute | solution.py:51
  57.9 6.9 %collective-permute-start.9 = (f32[320,1]{0,1:T(1,128)S(1)}, f32[320,1]{0,1:T(1,128)S(1)}, u32[]{:S(2)}, u32[]{:S(2)}) collective-permute-start(f32[320,1]{0,1:T(1,128)S(1)} %get-tuple-element.103), channel_id=1, source_target_pairs={{0,8},{8,16},{16,24},{24,32},{32,40},{40,48},{48,56},{56,64},{64,7... | collective-permute-start | bytes 3848 | tf_op jit(solution)/shard_map/ppermute | solution.py:50
  58.0 4.9 %collective-permute-start.11 = (f32[1,128]{0,1:T(8,128)S(1)}, f32[1,128]{0,1:T(8,128)S(1)}, u32[]{:S(2)}, u32[]{:S(2)}) collective-permute-start(f32[1,128]{0,1:T(8,128)S(1)} %get-tuple-element.102), channel_id=1, source_target_pairs={{0,1},{1,2},{2,3},{3,4},{4,5},{5,6},{6,7},{7,0},{8,9},{9,10},{10,1... | collective-permute-start | bytes 1544 | tf_op jit(solution)/shard_map/ppermute | solution.py:50
  58.0 4.9 %collective-permute-start.10 = (f32[1,128]{0,1:T(8,128)S(1)}, f32[1,128]{0,1:T(8,128)S(1)}, u32[]{:S(2)}, u32[]{:S(2)}) collective-permute-start(f32[1,128]{0,1:T(8,128)S(1)} %get-tuple-element.101), channel_id=1, source_target_pairs={{1,0},{2,1},{3,2},{4,3},{5,4},{6,5},{7,6},{0,7},{9,8},{10,9},{11,1... | collective-permute-start | bytes 1544 | tf_op jit(solution)/shard_map/ppermute | solution.py:51
  101.2 7.1 %collective-permute-start.12 = (f32[320,1]{0,1:T(1,128)S(1)}, f32[320,1]{0,1:T(1,128)S(1)}, u32[]{:S(2)}, u32[]{:S(2)}) collective-permute-start(f32[320,1]{0,1:T(1,128)S(1)} %get-tuple-element.100), channel_id=1, source_target_pairs={{8,0},{16,8},{24,16},{32,24},{40,32},{48,40},{56,48},{64,56},{72,6... | collective-permute-start | bytes 3848 | tf_op jit(solution)/shard_map/ppermute | solution.py:51
  101.3 7.0 %collective-permute-start.13 = (f32[320,1]{0,1:T(1,128)S(1)}, f32[320,1]{0,1:T(1,128)S(1)}, u32[]{:S(2)}, u32[]{:S(2)}) collective-permute-start(f32[320,1]{0,1:T(1,128)S(1)} %get-tuple-element.99), channel_id=1, source_target_pairs={{0,8},{8,16},{16,24},{24,32},{32,40},{40,48},{48,56},{56,64},{64,7... | collective-permute-start | bytes 3848 | tf_op jit(solution)/shard_map/ppermute | solution.py:50
  103.4 4.9 %collective-permute-start.15 = (f32[1,128]{0,1:T(8,128)S(1)}, f32[1,128]{0,1:T(8,128)S(1)}, u32[]{:S(2)}, u32[]{:S(2)}) collective-permute-start(f32[1,128]{0,1:T(8,128)S(1)} %get-tuple-element.98), channel_id=1, source_target_pairs={{0,1},{1,2},{2,3},{3,4},{4,5},{5,6},{6,7},{7,0},{8,9},{9,10},{10,1... | collective-permute-start | bytes 1544 | tf_op jit(solution)/shard_map/ppermute | solution.py:50
  103.4 4.9 %collective-permute-start.14 = (f32[1,128]{0,1:T(8,128)S(1)}, f32[1,128]{0,1:T(8,128)S(1)}, u32[]{:S(2)}, u32[]{:S(2)}) collective-permute-start(f32[1,128]{0,1:T(8,128)S(1)} %get-tuple-element.97), channel_id=1, source_target_pairs={{1,0},{2,1},{3,2},{4,3},{5,4},{6,5},{7,6},{0,7},{9,8},{10,9},{11,1... | collective-permute-start | bytes 1544 | tf_op jit(solution)/shard_map/ppermute | solution.py:51
  150.3 7.0 %collective-permute-start.16 = (f32[320,1]{0,1:T(1,128)S(1)}, f32[320,1]{0,1:T(1,128)S(1)}, u32[]{:S(2)}, u32[]{:S(2)}) collective-permute-start(f32[320,1]{0,1:T(1,128)S(1)} %get-tuple-element.96), channel_id=1, source_target_pairs={{8,0},{16,8},{24,16},{32,24},{40,32},{48,40},{56,48},{64,56},{72,6... | collective-permute-start | bytes 3848 | tf_op jit(solution)/shard_map/ppermute | solution.py:51
  151.0 6.9 %collective-permute-start.17 = (f32[320,1]{0,1:T(1,128)S(1)}, f32[320,1]{0,1:T(1,128)S(1)}, u32[]{:S(2)}, u32[]{:S(2)}) collective-permute-start(f32[320,1]{0,1:T(1,128)S(1)} %get-tuple-element.95), channel_id=1, source_target_pairs={{0,8},{8,16},{16,24},{24,32},{32,40},{40,48},{48,56},{56,64},{64,7... | collective-permute-start | bytes 3848 | tf_op jit(solution)/shard_map/ppermute | solution.py:50
  152.3 4.9 %collective-permute-start.19 = (f32[1,128]{0,1:T(8,128)S(1)}, f32[1,128]{0,1:T(8,128)S(1)}, u32[]{:S(2)}, u32[]{:S(2)}) collective-permute-start(f32[1,128]{0,1:T(8,128)S(1)} %get-tuple-element.94), channel_id=1, source_target_pairs={{0,1},{1,2},{2,3},{3,4},{4,5},{5,6},{6,7},{7,0},{8,9},{9,10},{10,1... | collective-permute-start | bytes 1544 | tf_op jit(solution)/shard_map/ppermute | solution.py:50
  152.3 4.9 %collective-permute-start.18 = (f32[1,128]{0,1:T(8,128)S(1)}, f32[1,128]{0,1:T(8,128)S(1)}, u32[]{:S(2)}, u32[]{:S(2)}) collective-permute-start(f32[1,128]{0,1:T(8,128)S(1)} %get-tuple-element.93), channel_id=1, source_target_pairs={{1,0},{2,1},{3,2},{4,3},{5,4},{6,5},{7,6},{0,7},{9,8},{10,9},{11,1... | collective-permute-start | bytes 1544 | tf_op jit(solution)/shard_map/ppermute | solution.py:51
  197.2 10.5 %collective-permute-start.23 = (f32[1,128]{0,1:T(8,128)S(1)}, f32[1,128]{0,1:T(8,128)S(1)}, u32[]{:S(2)}, u32[]{:S(2)}) collective-permute-start(f32[1,128]{0,1:T(8,128)S(1)} %get-tuple-element.90), channel_id=1, source_target_pairs={{0,1},{1,2},{2,3},{3,4},{4,5},{5,6},{6,7},{7,0},{8,9},{9,10},{10,1... | collective-permute-start | bytes 1544 | tf_op jit(solution)/shard_map/ppermute | solution.py:50
  197.4 10.3 %collective-permute-start.20 = (f32[320,1]{0,1:T(1,128)S(1)}, f32[320,1]{0,1:T(1,128)S(1)}, u32[]{:S(2)}, u32[]{:S(2)}) collective-permute-start(f32[320,1]{0,1:T(1,128)S(1)} %get-tuple-element.92), channel_id=1, source_target_pairs={{8,0},{16,8},{24,16},{32,24},{40,32},{48,40},{56,48},{64,56},{72,6... | collective-permute-start | bytes 3848 | tf_op jit(solution)/shard_map/ppermute | solution.py:51
  197.5 10.1 %collective-permute-start.21 = (f32[320,1]{0,1:T(1,128)S(1)}, f32[320,1]{0,1:T(1,128)S(1)}, u32[]{:S(2)}, u32[]{:S(2)}) collective-permute-start(f32[320,1]{0,1:T(1,128)S(1)} %get-tuple-element.91), channel_id=1, source_target_pairs={{0,8},{8,16},{16,24},{24,32},{32,40},{40,48},{48,56},{56,64},{64,7... | collective-permute-start | bytes 3848 | tf_op jit(solution)/shard_map/ppermute | solution.py:50
  199.4 8.3 %collective-permute-start.22 = (f32[1,128]{0,1:T(8,128)S(1)}, f32[1,128]{0,1:T(8,128)S(1)}, u32[]{:S(2)}, u32[]{:S(2)}) collective-permute-start(f32[1,128]{0,1:T(8,128)S(1)} %get-tuple-element.89), channel_id=1, source_target_pairs={{1,0},{2,1},{3,2},{4,3},{5,4},{6,5},{7,6},{0,7},{9,8},{10,9},{11,1... | collective-permute-start | bytes 1544 | tf_op jit(solution)/shard_map/ppermute | solution.py:51
  248.3 10.5 %collective-permute-start.26 = (f32[1,128]{0,1:T(8,128)}, f32[1,128]{0,1:T(8,128)}, u32[]{:S(2)}, u32[]{:S(2)}) collective-permute-start(f32[1,128]{0,1:T(8,128)} %slice.452), channel_id=1, source_target_pairs={{1,0},{2,1},{3,2},{4,3},{5,4},{6,5},{7,6},{0,7},{9,8},{10,9},{11,1... | collective-permute-start | bytes 1544 | tf_op jit(solution)/shard_map/ppermute | solution.py:51
  249.3 9.5 %collective-permute-start.24 = (f32[320,1]{0,1:T(1,128)}, f32[320,1]{0,1:T(1,128)S(1)}, u32[]{:S(2)}, u32[]{:S(2)}) collective-permute-start(f32[320,1]{0,1:T(1,128)} %get-tuple-element.87), channel_id=1, source_target_pairs={{8,0},{16,8},{24,16},{32,24},{40,32},{48,40},{56,48},{64,56},{72,6... | collective-permute-start | bytes 3848 | tf_op jit(solution)/shard_map/ppermute | solution.py:51
  249.3 9.5 %collective-permute-start.25 = (f32[320,1]{0,1:T(1,128)}, f32[320,1]{0,1:T(1,128)S(1)}, u32[]{:S(2)}, u32[]{:S(2)}) collective-permute-start(f32[320,1]{0,1:T(1,128)} %get-tuple-element.86), channel_id=1, source_target_pairs={{0,8},{8,16},{16,24},{24,32},{32,40},{40,48},{48,56},{56,64},{64,7... | collective-permute-start | bytes 3848 | tf_op jit(solution)/shard_map/ppermute | solution.py:50
  (24 other events, 217.0 us)
where the time goes:
time: 267 us; the launch traced here: 266 us
  blocking collectives  131 us (49%)
  starting transfers between devices  43.2 us (16%)
  other arithmetic  38.9 us (15%)
  local copies, waits for them, and re-layouts  30.2 us (11%)
  between operations  14.8 us (6%)
  waiting for transfers between devices  8.19 us (3%)
    psum x16, blocking collectives, one_axis_at_a_time(): x = lax.psum(x, axis)  131 us
    ppermute x12, starting transfers between devices, padded_3(): lax.ppermute(first, axis, [(b, a) for a, b in up])  26.7 us
    unnamed x69, local copies, waits for them, and re-layouts  14.5 us
    ppermute x2, starting transfers between devices, padded_2(): lax.ppermute(head, axis, [((i + 1) % count, i) for i in range(count)])  9.01 us
    reduce_sum x1, other arithmetic, on_device(): east_flow = wet_cycle * jnp.sum(thick * u_star, 0)  8.32 us
    ppermute x11, waiting for transfers between devices, padded_3(): lax.ppermute(last, axis, up)  7.52 us
    reduce_sum x4, other arithmetic, pair_totals(): jnp.sum(precond * image)  7.51 us
    ppermute x11, starting transfers between devices, padded_3(): lax.ppermute(last, axis, up)  7.45 us
  transfers between devices with their start and end apart: 27, of which 6 were waited for; matrix products, arithmetic and copies ran while one was open for 14% of the time, Pallas kernels for 0%

commit v1 on v0

--- a/solution.py
+++ b/solution.py
@@ -19,7 +19,7 @@
 
 def one_axis_at_a_time(x, axes):
     for axis in axes:
-        x = lax.psum(x, axis)
+        x = jnp.sum(lax.all_gather(x, axis), axis=0)
     return x
 
 

time: 267 us -> 353 us (1.32)
  local copies, waits for them, and re-layouts: 30.2 us -> 98.9 us
  other arithmetic: 38.9 us -> 62.4 us
  blocking collectives: 131 us -> 122 us
    psum x16 -> x0, blocking collectives: 131 us -> none  [one_axis_at_a_time(): x = lax.psum(x, axis)]
    unnamed x0 -> x16, blocking collectives: none -> 122 us
    unnamed x69 -> x159, local copies, waits for them, and re-layouts: 14.5 us -> 81.7 us
    reduce_sum x0 -> x32, other arithmetic: none -> 20.2 us  [one_axis_at_a_time(): x = jnp.sum(lax.all_gather(x, axis), axis=0)]
  transfers between devices with their start and end apart: 27 -> 27, of which waited for: 6 -> 9; matrix products, arithmetic and copies ran while one was open for 14% -> 10% of each run, Pallas kernels for 0% -> 0%
where the time goes in v1:
time: 353 us; the launch traced here: 351 us
  blocking collectives  122 us (35%)
  local copies, waits for them, and re-layouts  98.9 us (28%)
  other arithmetic  62.4 us (18%)
  starting transfers between devices  43.2 us (12%)
  between operations  15.2 us (4%)
  waiting for transfers between devices  9.18 us (3%)
    unnamed x16, blocking collectives  122 us
    unnamed x159, local copies, waits for them, and re-layouts  81.7 us
    ppermute x12, starting transfers between devices, padded_3(): lax.ppermute(first, axis, [(b, a) for a, b in up])  27 us
    reduce_sum x32, other arithmetic, one_axis_at_a_time(): x = jnp.sum(lax.all_gather(x, axis), axis=0)  20.2 us
    reduce_sum x4, other arithmetic, pair_totals(): jnp.sum(precond * image)  10.4 us
    ppermute x2, starting transfers between devices, padded_2(): lax.ppermute(head, axis, [((i + 1) % count, i) for i in range(count)])  8.99 us
    reduce_sum x1, other arithmetic, on_device(): east_flow = wet_cycle * jnp.sum(thick * u_star, 0)  8.29 us
    ppermute x11, starting transfers between devices, padded_3(): lax.ppermute(last, axis, up)  7.22 us
  transfers between devices with their start and end apart: 27, of which 9 were waited for; matrix products, arithmetic and copies ran while one was open for 10% of the time, Pallas kernels for 0%

profile of v1, /device:TPU:0, one launch (start us, length us, event | category | flops | bytes accessed | tf_op | source)
XLA Modules:
  0.0 350.5 jit_solution(1451367002350614986)
XLA Ops:
  9.5 6.7 %collective-permute-start.1 = (f32[13,320,2]{1,2,0:T(2,128)S(1)}, f32[13,320,2]{1,2,0:T(2,128)S(1)}, u32[]{:S(2)}, u32[]{:S(2)}) collective-permute-start(f32[13,320,2]{1,2,0:T(2,128)S(1)} %get-tuple-element.73), channel_id=1, source_target_pairs={{8,0},{16,8},{24,16},{32,24},{40,32},{48,40},{56,48},{64,56},{72,6... | collective-permute-start | bytes 99848 | tf_op jit(solution)/shard_map/ppermute | solution.py:35
  16.8 5.3 %collective-permute-start.4 = (f32[320,1]{0,1:T(1,128)}, f32[320,1]{0,1:T(1,128)}, u32[]{:S(2)}, u32[]{:S(2)}) collective-permute-start(f32[320,1]{0,1:T(1,128)} %get-tuple-element.108), channel_id=1, source_target_pairs={{8,0},{16,8},{24,16},{32,24},{40,32},{48,40},{56,48},{64,56},{72,6... | collective-permute-start | bytes 3848 | tf_op jit(solution)/shard_map/ppermute | solution.py:51
  32.7 3.0 collective-permute-start.6
  42.4 8.3 %multiply_reduce_fusion.1 = (f32[322,130]{0,1:T(8,128)S(1)}, f32[322,130]{0,1:T(8,128)S(1)}, f32[4,322,130]{1,2,0:T(8,128)}, f32[4,322,130]{1,2,0:T(8,128)}) fusion(f32[4]{0:T(128)S(1)} %copy-done.24, f32[13,324,132]{1,2,0:T(8,128)S(1)} %pad_maximum_fusion, f32[322]{0:T(512)S(1)} %fusion.91, f32[13,320,2]{1,2,0:T(2,128)S(1)} %collective-permute-done.1, ...), kind=kLoop, calls=%fused_computation.40 | loop fusion | flops 10632440 | bytes 9592600 | tf_op jit(solution)/shard_map/reduce_sum | solution.py:181
  53.1 5.4 %collective-permute-start.8 = (f32[320,1]{0,1:T(1,128)S(1)}, f32[320,1]{0,1:T(1,128)}, u32[]{:S(2)}, u32[]{:S(2)}) collective-permute-start(f32[320,1]{0,1:T(1,128)S(1)} %get-tuple-element.104), channel_id=1, source_target_pairs={{8,0},{16,8},{24,16},{32,24},{40,32},{48,40},{56,48},{64,56},{72,6... | collective-permute-start | bytes 3848 | tf_op jit(solution)/shard_map/ppermute | solution.py:51
  59.2 3.0 collective-permute-start.10
  65.5 3.3 multiply_reduce_fusion.7
  73.3 7.8 %all-reduce.60 = (f32[4]{0:T(128)S(1)}, f32[4]{0:T(128)S(1)}) all-reduce(f32[4]{0:T(128)} %copy-done.25, f32[4]{0:T(128)} %copy-done.26), channel_id=1, replica_groups=mesh['gx_0'=4,'gx_1'=4,'gy_0'=4,'gy_1'=2] {'gx_0'}, use_global_device_ids=true, to_apply=%add.17 | all-reduce | flops 8 | bytes 64
  87.0 12.7 %all-reduce.56 = (f32[4]{0:T(128)S(1)}, f32[4]{0:T(128)S(1)}) all-reduce(f32[4]{0:T(128)} %copy-done.27, f32[4]{0:T(128)} %copy-done.28), channel_id=1, replica_groups=mesh['gx_0'=4,'gx_1'=4,'gy_0'=4,'gy_1'=2] {'gx_1'}, use_global_device_ids=true, to_apply=%add.18 | all-reduce | flops 8 | bytes 64
  105.7 7.8 %all-reduce.52 = (f32[4]{0:T(128)S(1)}, f32[4]{0:T(128)S(1)}) all-reduce(f32[4]{0:T(128)} %copy-done.29, f32[4]{0:T(128)} %copy-done.30), channel_id=1, replica_groups=mesh['gx_0'=4,'gx_1'=4,'gy_0'=4,'gy_1'=2] {'gy_0'}, use_global_device_ids=true, to_apply=%add.19 | all-reduce | flops 8 | bytes 64
  116.7 2.6 dynamic-update-slice.7
  119.3 2.6 all-reduce.64
  127.7 3.0 collective-permute-start.14
  132.6 3.0 multiply_reduce_fusion.5
  137.5 2.5 dynamic-update-slice.12
  140.0 7.8 %all-reduce.59 = (f32[4]{0:T(128)S(1)}, f32[4]{0:T(128)S(1)}) all-reduce(f32[4]{0:T(128)} %copy-done.32, f32[4]{0:T(128)} %dynamic-update-slice.12), channel_id=1, replica_groups=mesh['gx_0'=4,'gx_1'=4,'gy_0'=4,'gy_1'=2] {'gx_0'}, use_global_device_ids=true, to_apply=%add.25 | all-reduce | flops 8 | bytes 64
  153.6 11.8 %all-reduce.55 = (f32[4]{0:T(128)S(1)}, f32[4]{0:T(128)S(1)}) all-reduce(f32[4]{0:T(128)} %copy-done.33, f32[4]{0:T(128)} %dynamic-update-slice.13), channel_id=1, replica_groups=mesh['gx_0'=4,'gx_1'=4,'gy_0'=4,'gy_1'=2] {'gx_1'}, use_global_device_ids=true, to_apply=%add.26 | all-reduce | flops 8 | bytes 64
  168.7 2.6 dynamic-update-slice.14
  171.3 8.6 %all-reduce.51 = (f32[4]{0:T(128)S(1)}, f32[4]{0:T(128)S(1)}) all-reduce(f32[4]{0:T(128)} %copy-done.34, f32[4]{0:T(128)} %dynamic-update-slice.14), channel_id=1, replica_groups=mesh['gx_0'=4,'gx_1'=4,'gy_0'=4,'gy_1'=2] {'gy_0'}, use_global_device_ids=true, to_apply=%add.27 | all-reduce | flops 8 | bytes 64
  185.7 2.6 all-reduce.63
  197.8 3.0 collective-permute-start.18
  206.9 2.6 dynamic-update-slice.20
  209.5 7.8 %all-reduce.58 = (f32[4]{0:T(128)S(1)}, f32[4]{0:T(128)S(1)}) all-reduce(f32[4]{0:T(128)} %copy-done.36, f32[4]{0:T(128)} %dynamic-update-slice.20), channel_id=1, replica_groups=mesh['gx_0'=4,'gx_1'=4,'gy_0'=4,'gy_1'=2] {'gx_0'}, use_global_device_ids=true, to_apply=%add.33 | all-reduce | flops 8 | bytes 64
  222.8 11.8 %all-reduce.54 = (f32[4]{0:T(128)S(1)}, f32[4]{0:T(128)S(1)}) all-reduce(f32[4]{0:T(128)} %copy-done.37, f32[4]{0:T(128)} %dynamic-update-slice.21), channel_id=1, replica_groups=mesh['gx_0'=4,'gx_1'=4,'gy_0'=4,'gy_1'=2] {'gx_1'}, use_global_device_ids=true, to_apply=%add.34 | all-reduce | flops 8 | bytes 64
  240.2 7.8 %all-reduce.50 = (f32[4]{0:T(128)S(1)}, f32[4]{0:T(128)S(1)}) all-reduce(f32[4]{0:T(128)} %copy-done.38, f32[4]{0:T(128)} %dynamic-update-slice.22), channel_id=1, replica_groups=mesh['gx_0'=4,'gx_1'=4,'gy_0'=4,'gy_1'=2] {'gy_0'}, use_global_device_ids=true, to_apply=%add.35 | all-reduce | flops 8 | bytes 64
  253.5 2.6 all-reduce.62
  276.9 7.7 %all-reduce.57 = (f32[4]{0:T(128)S(1)}, f32[4]{0:T(128)S(1)}) all-reduce(f32[4]{0:T(128)S(1)} %dynamic-update-slice.24, f32[4]{0:T(128)S(1)} %dynamic-update-slice.28), channel_id=1, replica_groups=mesh['gx_0'=4,'gx_1'=4,'gy_0'=4,'gy_1'=2] {'gx_0'}, use_global_device_ids=true, to_apply=%add.41 | all-reduce | flops 8 | bytes 64
  290.3 11.0 %all-reduce.53 = (f32[4]{0:T(128)S(1)}, f32[4]{0:T(128)S(1)}) all-reduce(f32[4]{0:T(128)S(1)} %dynamic-update-slice.25, f32[4]{0:T(128)S(1)} %dynamic-update-slice.29), channel_id=1, replica_groups=mesh['gx_0'=4,'gx_1'=4,'gy_0'=4,'gy_1'=2] {'gx_1'}, use_global_device_ids=true, to_apply=%add.42 | all-reduce | flops 8 | bytes 64
  307.1 8.5 %all-reduce.49 = (f32[4]{0:T(128)S(1)}, f32[4]{0:T(128)S(1)}) all-reduce(f32[4]{0:T(128)S(1)} %dynamic-update-slice.26, f32[4]{0:T(128)S(1)} %dynamic-update-slice.30), channel_id=1, replica_groups=mesh['gx_0'=4,'gx_1'=4,'gy_0'=4,'gy_1'=2] {'gy_0'}, use_global_device_ids=true, to_apply=%add.43 | all-reduce | flops 8 | bytes 64
  321.5 2.7 all-reduce.61
  334.9 4.4 %multiply_add_fusion = f32[4,320,128]{1,2,0:T(8,128)} fusion(f32[4,320,128]{1,2,0:T(8,128)S(1)} %copy.40, f32[4,320,128]{1,2,0:T(8,128)S(1)} %copy.39, f32[4,320,128]{1,2,0:T(8,128)S(1)} %copy.38, f32[13,320,2]{1,2,0:T(2,128)S(1)} %collective-permute-done.1, f32[1,320,128]{1,2,0:T(8,128)} %copy-done.9, f32[13,320,2]{1,2,0:T(2,128)S(1)} %collective-permute-done, ...), kind=kLoop, calls=%fused_computation.67 | loop fusion | flops 7536640 | bytes 4191296 | tf_op jit(solution)/shard_map/add | solution.py:211
  343.5 2.6 fusion.25
  (280 shorter events, 152.6 us)
Async XLA Ops:
  9.5 13.4 %copy-start.13 = (f32[320,128]{0,1:T(8,128)}, f32[320,128]{0,1:T(8,128)S(1)}, u32[]{:S(2)}) copy-start(f32[320,128]{0,1:T(8,128)S(1)} %get-tuple-element.82) | copy-start | bytes 491524
  9.5 32.8 %copy-start.9 = (f32[1,320,128]{1,2,0:T(8,128)}, f32[1,320,128]{1,2,0:T(8,128)S(1)}, u32[]{:S(2)}) copy-start(f32[1,320,128]{1,2,0:T(8,128)S(1)} %get-tuple-element.83) | copy-start | bytes 491524
  9.5 13.3 %collective-permute-start.1 = (f32[13,320,2]{1,2,0:T(2,128)S(1)}, f32[13,320,2]{1,2,0:T(2,128)S(1)}, u32[]{:S(2)}, u32[]{:S(2)}) collective-permute-start(f32[13,320,2]{1,2,0:T(2,128)S(1)} %get-tuple-element.73), channel_id=1, source_target_pairs={{8,0},{16,8},{24,16},{32,24},{40,32},{48,40},{56,48},{64,56},{72,6... | collective-permute-start | bytes 99848 | tf_op jit(solution)/shard_map/ppermute | solution.py:35
  16.2 7.3 %collective-permute-start = (f32[13,320,2]{1,2,0:T(2,128)S(1)}, f32[13,320,2]{1,2,0:T(2,128)S(1)}, u32[]{:S(2)}, u32[]{:S(2)}) collective-permute-start(f32[13,320,2]{1,2,0:T(2,128)S(1)} %get-tuple-element.72), channel_id=1, source_target_pairs={{0,8},{8,16},{16,24},{24,32},{32,40},{40,48},{48,56},{56,64},{64,7... | collective-permute-start | bytes 99848 | tf_op jit(solution)/shard_map/ppermute | solution.py:33
  16.8 34.0 %collective-permute-start.4 = (f32[320,1]{0,1:T(1,128)}, f32[320,1]{0,1:T(1,128)}, u32[]{:S(2)}, u32[]{:S(2)}) collective-permute-start(f32[320,1]{0,1:T(1,128)} %get-tuple-element.108), channel_id=1, source_target_pairs={{8,0},{16,8},{24,16},{32,24},{40,32},{48,40},{56,48},{64,56},{72,6... | collective-permute-start | bytes 3848 | tf_op jit(solution)/shard_map/ppermute | solution.py:51
  22.1 28.7 %collective-permute-start.5 = (f32[320,1]{0,1:T(1,128)}, f32[320,1]{0,1:T(1,128)}, u32[]{:S(2)}, u32[]{:S(2)}) collective-permute-start(f32[320,1]{0,1:T(1,128)} %get-tuple-element.107), channel_id=1, source_target_pairs={{0,8},{8,16},{16,24},{24,32},{32,40},{40,48},{48,56},{56,64},{64,7... | collective-permute-start | bytes 3848 | tf_op jit(solution)/shard_map/ppermute | solution.py:50
  22.8 28.0 %collective-permute-start.7 = (f32[1,128]{0,1:T(8,128)}, f32[1,128]{0,1:T(8,128)}, u32[]{:S(2)}, u32[]{:S(2)}) collective-permute-start(f32[1,128]{0,1:T(8,128)} %get-tuple-element.106), channel_id=1, source_target_pairs={{0,1},{1,2},{2,3},{3,4},{4,5},{5,6},{6,7},{7,0},{8,9},{9,10},{10,1... | collective-permute-start | bytes 1544 | tf_op jit(solution)/shard_map/ppermute | solution.py:50
  27.1 5.7 %collective-permute-start.3 = (f32[13,2,132]{2,1,0:T(2,128)}, f32[13,2,132]{2,1,0:T(2,128)}, u32[]{:S(2)}, u32[]{:S(2)}) collective-permute-start(f32[13,2,132]{2,1,0:T(2,128)} %copy.42), channel_id=1, source_target_pairs={{1,0},{2,1},{3,2},{4,3},{5,4},{6,5},{7,6},{0,7},{9,8},{10,9},{11,1... | collective-permute-start | bytes 41192 | tf_op jit(solution)/shard_map/ppermute | solution.py:35
  30.5 6.3 %collective-permute-start.2 = (f32[13,2,132]{2,1,0:T(2,128)}, f32[13,2,132]{2,1,0:T(2,128)}, u32[]{:S(2)}, u32[]{:S(2)}) collective-permute-start(f32[13,2,132]{2,1,0:T(2,128)} %copy.41), channel_id=1, source_target_pairs={{0,1},{1,2},{2,3},{3,4},{4,5},{5,6},{6,7},{7,0},{8,9},{9,10},{10,1... | collective-permute-start | bytes 41192 | tf_op jit(solution)/shard_map/ppermute | solution.py:33
  32.7 18.1 %collective-permute-start.6 = (f32[1,128]{0,1:T(8,128)}, f32[1,128]{0,1:T(8,128)}, u32[]{:S(2)}, u32[]{:S(2)}) collective-permute-start(f32[1,128]{0,1:T(8,128)} %get-tuple-element.105), channel_id=1, source_target_pairs={{1,0},{2,1},{3,2},{4,3},{5,4},{6,5},{7,6},{0,7},{9,8},{10,9},{11,1... | collective-permute-start | bytes 1544 | tf_op jit(solution)/shard_map/ppermute | solution.py:51
  53.1 11.3 %collective-permute-start.8 = (f32[320,1]{0,1:T(1,128)S(1)}, f32[320,1]{0,1:T(1,128)}, u32[]{:S(2)}, u32[]{:S(2)}) collective-permute-start(f32[320,1]{0,1:T(1,128)S(1)} %get-tuple-element.104), channel_id=1, source_target_pairs={{8,0},{16,8},{24,16},{32,24},{40,32},{48,40},{56,48},{64,56},{72,6... | collective-permute-start | bytes 3848 | tf_op jit(solution)/shard_map/ppermute | solution.py:51
  58.5 7.0 %collective-permute-start.9 = (f32[320,1]{0,1:T(1,128)S(1)}, f32[320,1]{0,1:T(1,128)}, u32[]{:S(2)}, u32[]{:S(2)}) collective-permute-start(f32[320,1]{0,1:T(1,128)S(1)} %get-tuple-element.103), channel_id=1, source_target_pairs={{0,8},{8,16},{16,24},{24,32},{32,40},{40,48},{48,56},{56,64},{64,7... | collective-permute-start | bytes 3848 | tf_op jit(solution)/shard_map/ppermute | solution.py:50
  59.2 5.2 %collective-permute-start.11 = (f32[1,128]{0,1:T(8,128)}, f32[1,128]{0,1:T(8,128)}, u32[]{:S(2)}, u32[]{:S(2)}) collective-permute-start(f32[1,128]{0,1:T(8,128)} %get-tuple-element.102), channel_id=1, source_target_pairs={{0,1},{1,2},{2,3},{3,4},{4,5},{5,6},{6,7},{7,0},{8,9},{9,10},{10,1... | collective-permute-start | bytes 1544 | tf_op jit(solution)/shard_map/ppermute | solution.py:50
  59.2 5.2 %collective-permute-start.10 = (f32[1,128]{0,1:T(8,128)}, f32[1,128]{0,1:T(8,128)}, u32[]{:S(2)}, u32[]{:S(2)}) collective-permute-start(f32[1,128]{0,1:T(8,128)} %get-tuple-element.101), channel_id=1, source_target_pairs={{1,0},{2,1},{3,2},{4,3},{5,4},{6,5},{7,6},{0,7},{9,8},{10,9},{11,1... | collective-permute-start | bytes 1544 | tf_op jit(solution)/shard_map/ppermute | solution.py:51
  125.4 10.1 %copy-start.18 = (f32[320,128]{0,1:T(8,128)}, f32[320,128]{0,1:T(8,128)S(1)}, u32[]{:S(2)}) copy-start(f32[320,128]{0,1:T(8,128)S(1)} %get-tuple-element.61) | copy-start | bytes 491524
  125.5 7.1 %collective-permute-start.12 = (f32[320,1]{0,1:T(1,128)S(1)}, f32[320,1]{0,1:T(1,128)S(1)}, u32[]{:S(2)}, u32[]{:S(2)}) collective-permute-start(f32[320,1]{0,1:T(1,128)S(1)} %get-tuple-element.100), channel_id=1, source_target_pairs={{8,0},{16,8},{24,16},{32,24},{40,32},{48,40},{56,48},{64,56},{72,6... | collective-permute-start | bytes 3848 | tf_op jit(solution)/shard_map/ppermute | solution.py:51
  125.6 7.0 %collective-permute-start.13 = (f32[320,1]{0,1:T(1,128)S(1)}, f32[320,1]{0,1:T(1,128)S(1)}, u32[]{:S(2)}, u32[]{:S(2)}) collective-permute-start(f32[320,1]{0,1:T(1,128)S(1)} %get-tuple-element.99), channel_id=1, source_target_pairs={{0,8},{8,16},{16,24},{24,32},{32,40},{40,48},{48,56},{56,64},{64,7... | collective-permute-start | bytes 3848 | tf_op jit(solution)/shard_map/ppermute | solution.py:50
  127.6 4.9 %collective-permute-start.15 = (f32[1,128]{0,1:T(8,128)S(1)}, f32[1,128]{0,1:T(8,128)S(1)}, u32[]{:S(2)}, u32[]{:S(2)}) collective-permute-start(f32[1,128]{0,1:T(8,128)S(1)} %get-tuple-element.98), channel_id=1, source_target_pairs={{0,1},{1,2},{2,3},{3,4},{4,5},{5,6},{6,7},{7,0},{8,9},{9,10},{10,1... | collective-permute-start | bytes 1544 | tf_op jit(solution)/shard_map/ppermute | solution.py:50
  127.7 4.9 %collective-permute-start.14 = (f32[1,128]{0,1:T(8,128)S(1)}, f32[1,128]{0,1:T(8,128)S(1)}, u32[]{:S(2)}, u32[]{:S(2)}) collective-permute-start(f32[1,128]{0,1:T(8,128)S(1)} %get-tuple-element.97), channel_id=1, source_target_pairs={{1,0},{2,1},{3,2},{4,3},{5,4},{6,5},{7,6},{0,7},{9,8},{10,9},{11,1... | collective-permute-start | bytes 1544 | tf_op jit(solution)/shard_map/ppermute | solution.py:51
  195.6 9.5 %copy-start.15 = (f32[320,128]{0,1:T(8,128)}, f32[320,128]{0,1:T(8,128)S(1)}, u32[]{:S(2)}) copy-start(f32[320,128]{0,1:T(8,128)S(1)} %get-tuple-element.57) | copy-start | bytes 491524
  195.7 7.0 %collective-permute-start.16 = (f32[320,1]{0,1:T(1,128)S(1)}, f32[320,1]{0,1:T(1,128)S(1)}, u32[]{:S(2)}, u32[]{:S(2)}) collective-permute-start(f32[320,1]{0,1:T(1,128)S(1)} %get-tuple-element.96), channel_id=1, source_target_pairs={{8,0},{16,8},{24,16},{32,24},{40,32},{48,40},{56,48},{64,56},{72,6... | collective-permute-start | bytes 3848 | tf_op jit(solution)/shard_map/ppermute | solution.py:51
  196.4 6.9 %collective-permute-start.17 = (f32[320,1]{0,1:T(1,128)S(1)}, f32[320,1]{0,1:T(1,128)S(1)}, u32[]{:S(2)}, u32[]{:S(2)}) collective-permute-start(f32[320,1]{0,1:T(1,128)S(1)} %get-tuple-element.95), channel_id=1, source_target_pairs={{0,8},{8,16},{16,24},{24,32},{32,40},{40,48},{48,56},{56,64},{64,7... | collective-permute-start | bytes 3848 | tf_op jit(solution)/shard_map/ppermute | solution.py:50
  197.8 4.9 %collective-permute-start.19 = (f32[1,128]{0,1:T(8,128)S(1)}, f32[1,128]{0,1:T(8,128)S(1)}, u32[]{:S(2)}, u32[]{:S(2)}) collective-permute-start(f32[1,128]{0,1:T(8,128)S(1)} %get-tuple-element.94), channel_id=1, source_target_pairs={{0,1},{1,2},{2,3},{3,4},{4,5},{5,6},{6,7},{7,0},{8,9},{9,10},{10,1... | collective-permute-start | bytes 1544 | tf_op jit(solution)/shard_map/ppermute | solution.py:50
  197.8 4.9 %collective-permute-start.18 = (f32[1,128]{0,1:T(8,128)S(1)}, f32[1,128]{0,1:T(8,128)S(1)}, u32[]{:S(2)}, u32[]{:S(2)}) collective-permute-start(f32[1,128]{0,1:T(8,128)S(1)} %get-tuple-element.93), channel_id=1, source_target_pairs={{1,0},{2,1},{3,2},{4,3},{5,4},{6,5},{7,6},{0,7},{9,8},{10,9},{11,1... | collective-permute-start | bytes 1544 | tf_op jit(solution)/shard_map/ppermute | solution.py:51
  262.8 9.7 %copy-start.16 = (f32[320,128]{0,1:T(8,128)}, f32[320,128]{0,1:T(8,128)S(1)}, u32[]{:S(2)}) copy-start(f32[320,128]{0,1:T(8,128)S(1)} %get-tuple-element.54) | copy-start | bytes 491524
  262.9 4.9 %collective-permute-start.23 = (f32[1,128]{0,1:T(8,128)S(1)}, f32[1,128]{0,1:T(8,128)S(1)}, u32[]{:S(2)}, u32[]{:S(2)}) collective-permute-start(f32[1,128]{0,1:T(8,128)S(1)} %get-tuple-element.90), channel_id=1, source_target_pairs={{0,1},{1,2},{2,3},{3,4},{4,5},{5,6},{6,7},{7,0},{8,9},{9,10},{10,1... | collective-permute-start | bytes 1544 | tf_op jit(solution)/shard_map/ppermute | solution.py:50
  263.1 6.2 %collective-permute-start.20 = (f32[320,1]{0,1:T(1,128)S(1)}, f32[320,1]{0,1:T(1,128)S(1)}, u32[]{:S(2)}, u32[]{:S(2)}) collective-permute-start(f32[320,1]{0,1:T(1,128)S(1)} %get-tuple-element.92), channel_id=1, source_target_pairs={{8,0},{16,8},{24,16},{32,24},{40,32},{48,40},{56,48},{64,56},{72,6... | collective-permute-start | bytes 3848 | tf_op jit(solution)/shard_map/ppermute | solution.py:51
  263.3 6.9 %collective-permute-start.21 = (f32[320,1]{0,1:T(1,128)S(1)}, f32[320,1]{0,1:T(1,128)S(1)}, u32[]{:S(2)}, u32[]{:S(2)}) collective-permute-start(f32[320,1]{0,1:T(1,128)S(1)} %get-tuple-element.91), channel_id=1, source_target_pairs={{0,8},{8,16},{16,24},{24,32},{32,40},{40,48},{48,56},{56,64},{64,7... | collective-permute-start | bytes 3848 | tf_op jit(solution)/shard_map/ppermute | solution.py:50
  265.1 4.1 %collective-permute-start.22 = (f32[1,128]{0,1:T(8,128)S(1)}, f32[1,128]{0,1:T(8,128)S(1)}, u32[]{:S(2)}, u32[]{:S(2)}) collective-permute-start(f32[1,128]{0,1:T(8,128)S(1)} %get-tuple-element.89), channel_id=1, source_target_pairs={{1,0},{2,1},{3,2},{4,3},{5,4},{6,5},{7,6},{0,7},{9,8},{10,9},{11,1... | collective-permute-start | bytes 1544 | tf_op jit(solution)/shard_map/ppermute | solution.py:51
  331.9 10.6 %collective-permute-start.26 = (f32[1,128]{0,1:T(8,128)}, f32[1,128]{0,1:T(8,128)}, u32[]{:S(2)}, u32[]{:S(2)}) collective-permute-start(f32[1,128]{0,1:T(8,128)} %slice.452), channel_id=1, source_target_pairs={{1,0},{2,1},{3,2},{4,3},{5,4},{6,5},{7,6},{0,7},{9,8},{10,9},{11,1... | collective-permute-start | bytes 1544 | tf_op jit(solution)/shard_map/ppermute | solution.py:51
  332.9 9.6 %collective-permute-start.24 = (f32[320,1]{0,1:T(1,128)}, f32[320,1]{0,1:T(1,128)S(1)}, u32[]{:S(2)}, u32[]{:S(2)}) collective-permute-start(f32[320,1]{0,1:T(1,128)} %get-tuple-element.87), channel_id=1, source_target_pairs={{8,0},{16,8},{24,16},{32,24},{40,32},{48,40},{56,48},{64,56},{72,6... | collective-permute-start | bytes 3848 | tf_op jit(solution)/shard_map/ppermute | solution.py:51
  333.1 9.3 %collective-permute-start.25 = (f32[320,1]{0,1:T(1,128)}, f32[320,1]{0,1:T(1,128)S(1)}, u32[]{:S(2)}, u32[]{:S(2)}) collective-permute-start(f32[320,1]{0,1:T(1,128)} %get-tuple-element.86), channel_id=1, source_target_pairs={{0,8},{8,16},{16,24},{24,32},{32,40},{40,48},{48,56},{56,64},{64,7... | collective-permute-start | bytes 3848 | tf_op jit(solution)/shard_map/ppermute | solution.py:50
  (35 other events, 156.3 us)
